TPU v7x, 32 devices: a whole 2x2x4 slice. The times are simulated.
32 devices in a mesh: row: 8 (over z, y), col: 4 (over x, core).
Axes of the slice: x: 2, y: 2, z: 4, core: 2. Of those that a mesh axis runs over, the one named last changes fastest.
Arguments:
- root_rhs: bfloat16 [8, 8192], replicated, may hold values from -6 to 6
- diag_inv: bfloat16 [16, 512, 512], replicated, may hold values from -1 to 2
- tile_u: bfloat16 [8, 4, 2, 4, 128, 512], P('row', 'col'), may hold values from -0.1875 to 0.1875
- tile_v: bfloat16 [8, 4, 2, 4, 512, 128], P('row', 'col'), may hold values from -0.25 to 0.25
- tile_rank: int32 [8, 4, 2, 4], P('row', 'col'), may hold values from 16 to 128
- child_x: bfloat16 [32, 8, 512], P(('row', 'col')), may hold values from -6 to 6
- border_t: bfloat16 [32, 512, 1024], P(('row', 'col')), may hold values from -0.09375 to 0.09375
- child_inv: bfloat16 [32, 512, 512], P(('row', 'col')), may hold values from -1 to 2
- child_blocks: int32 [32, 8], P(('row', 'col')), may hold values from 0 to 63
Outputs:
- root_solution: float32 [8, 8192], P(None, ('row', 'col'))
- child_out: float32 [32, 8, 512], P(('row', 'col'))
All inputs are finite; a program needn't handle non-finite values.
Results may differ from a plain program's by a relative error of at most 0.017.
Values sent between devices are 32-bit elements; how exact they have to be, the bound alone decides.
A program may use at most 64 MiB of HBM per device.

v0:
```python
import jax
import jax.numpy as jnp
from jax import lax
from jax.sharding import PartitionSpec as P

BLK = 128
BB = 8


def per_device(
    root_rhs, diag_inv, tile_u, tile_v, tile_rank, child_x, border_t, child_inv, child_blocks
):
    highest_precision = lax.Precision.HIGHEST
    n_row = lax.axis_size("row")
    n_col = lax.axis_size("col")
    my_row = lax.axis_index("row")
    my_col = lax.axis_index("col")
    ntile = diag_inv.shape[0]
    tile = diag_inv.shape[1]
    rhs_count = root_rhs.shape[0]
    rank_max = tile_u.shape[4]
    t_rows = tile_u.shape[2]
    t_cols = tile_u.shape[3]
    left_tiles = tile_u[0, 0]
    right_tiles = tile_v[0, 0]
    tile_ranks = tile_rank[0, 0]
    blocks_per_front = tile // BLK
    n_child = child_x.shape[0]
    upward = jnp.einsum("crs,csb->crb", child_x, border_t, preferred_element_type=jnp.float32)
    pieces = (
        upward.reshape(n_child, rhs_count, BB, BLK)
        .transpose(1, 0, 2, 3)
        .reshape(rhs_count, n_child * BB, BLK)
    )
    flat_blocks = child_blocks.reshape(-1)
    dense_sum = (
        jnp.zeros((rhs_count, ntile * blocks_per_front, BLK), jnp.float32)
        .at[:, flat_blocks, :]
        .add(pieces)
    )
    dense_sum = dense_sum.reshape(rhs_count, ntile, tile)
    right_side = root_rhs.reshape(rhs_count, ntile, tile)
    col_ids = my_col + n_col * jnp.arange(t_cols)
    row_ids = my_row + n_row * jnp.arange(t_rows)
    rank_iota = jnp.arange(rank_max)

    def forward(column, solved_rows):
        owner_slot = column // n_row
        on_row = column % n_row == my_row
        known_cols = jnp.take(solved_rows, col_ids, axis=1).astype(jnp.bfloat16)
        right_row = lax.dynamic_index_in_dim(right_tiles, owner_slot, 0, keepdims=False)
        left_row_index = lax.dynamic_index_in_dim(left_tiles, owner_slot, 0, keepdims=False)
        rank_row = lax.dynamic_index_in_dim(tile_ranks, owner_slot, 0, keepdims=False)
        live_mask = (rank_iota[None, :] < rank_row[:, None]) & (col_ids[:, None] < column) & on_row
        coefficient_values = jnp.einsum(
            "rbt,btq->rbq", known_cols, right_row, preferred_element_type=jnp.float32
        )
        coefficient_values = jnp.where(live_mask[None], coefficient_values, 0.0).astype(
            jnp.bfloat16
        )
        partial_value = jnp.einsum(
            "rbq,bqt->rt", coefficient_values, left_row_index, preferred_element_type=jnp.float32
        )
        carried = lax.dynamic_index_in_dim(dense_sum, column, 1, keepdims=False)
        row_total = lax.psum(partial_value + carried, ("row", "col"))
        block_rhs = lax.dynamic_index_in_dim(right_side, column, 1, keepdims=False).astype(
            jnp.float32
        )
        inverse = lax.dynamic_index_in_dim(diag_inv, column, 0, keepdims=False).astype(jnp.float32)
        fresh = jnp.dot(block_rhs - row_total, inverse, precision=highest_precision)
        return lax.dynamic_update_index_in_dim(solved_rows, fresh, column, 1)

    solved_rows = lax.fori_loop(0, ntile, forward, jnp.zeros((rhs_count, ntile, tile), jnp.float32))

    def backward(sweep, result):
        column = ntile - 1 - sweep
        owner_slot = column // n_col
        on_col = column % n_col == my_col
        known_rows = jnp.take(result, row_ids, axis=1).astype(jnp.bfloat16)
        left_col = lax.dynamic_index_in_dim(left_tiles, owner_slot, 1, keepdims=False)
        right_col = lax.dynamic_index_in_dim(right_tiles, owner_slot, 1, keepdims=False)
        rank_col = lax.dynamic_index_in_dim(tile_ranks, owner_slot, 1, keepdims=False)
        live_mask = (rank_iota[None, :] < rank_col[:, None]) & (row_ids[:, None] > column) & on_col
        coefficient_values = jnp.einsum(
            "rat,aqt->raq", known_rows, left_col, preferred_element_type=jnp.float32
        )
        coefficient_values = jnp.where(live_mask[None], coefficient_values, 0.0).astype(
            jnp.bfloat16
        )
        partial_value = jnp.einsum(
            "raq,atq->rt", coefficient_values, right_col, preferred_element_type=jnp.float32
        )
        col_total = lax.psum(partial_value, ("row", "col"))
        block_solved = lax.dynamic_index_in_dim(solved_rows, column, 1, keepdims=False)
        inverse = lax.dynamic_index_in_dim(diag_inv, column, 0, keepdims=False).astype(jnp.float32)
        fresh = jnp.dot(block_solved - col_total, inverse.T, precision=highest_precision)
        return lax.dynamic_update_index_in_dim(result, fresh, column, 1)

    result = lax.fori_loop(0, ntile, backward, jnp.zeros((rhs_count, ntile, tile), jnp.float32))
    share = ntile * tile // (n_row * n_col)
    start = (my_row * n_col + my_col) * share
    root_part = lax.dynamic_slice_in_dim(result.reshape(rhs_count, ntile * tile), start, share, 1)
    gathered = result.reshape(rhs_count, ntile * blocks_per_front, BLK)[:, flat_blocks, :]
    gathered = gathered.reshape(rhs_count, n_child, BB * BLK).astype(jnp.bfloat16)
    returned = jnp.einsum("rcb,csb->crs", gathered, border_t, preferred_element_type=jnp.float32)
    child_out = child_x.astype(jnp.float32) - jnp.einsum(
        "crs,cst->crt", returned, child_inv.astype(jnp.float32), precision=highest_precision
    )
    return (root_part, child_out)


def solution(mesh):
    return jax.shard_map(
        per_device,
        mesh=mesh,
        in_specs=(
            P(),
            P(),
            P("row", "col", None, None, None, None),
            P("row", "col", None, None, None, None),
            P("row", "col", None, None),
            P(("row", "col"), None, None),
            P(("row", "col"), None, None),
            P(("row", "col"), None, None),
            P(("row", "col"), None),
        ),
        out_specs=(P(None, ("row", "col")), P(("row", "col"), None, None)),
        check_vma=False,
    )
```

profile of v0, /device:TPU:0, one launch (start us, length us, event | category | flops | bytes accessed | tf_op | source)
XLA Modules:
  0.0 1424.4 jit_solution(4886888711580385367)
XLA Ops:
  5.8 715.2 %while.32 = (s32[]{:T(128)}, f32[8,16,512]{2,0,1:T(8,128)S(1)}, bf16[8,16,512]{2,1,0:T(8,128)(2,1)S(1)}, s32[2,4]{1,0:T(2,128)}, s32[]{:T(128)}, /*index=5*/bf16...) while((s32[]{:T(128)}, f32[8,16,512]{2,0,1:T(8,128)S(1)}, ...), condition=%wide.region_3.4_spmd.clone, body=%wide.region_1.3_spmd.clone.sunk | while | flops 33598024 | bytes 1818560 | solution.py:73
  7.2 1.8 fusion.106
  9.0 42.0 %psum.32 = f32[8,512]{1,0:T(8,128)S(1)} all-reduce(f32[8,512]{1,0:T(8,128)S(1)} %fusion.106), channel_id=1, replica_groups=mesh['row'=8,'col'=4] {'row','col'}, use_global_device_ids=true, to_apply=%region_2.2 | all-reduce | flops 4096 | bytes 32768 | tf_op jit(solution)/shard_map/while/body/eval_jaxpr/psum | solution.py:65
  53.7 1.8 fusion.106
  55.5 40.2 %psum.32 = f32[8,512]{1,0:T(8,128)S(1)} all-reduce(f32[8,512]{1,0:T(8,128)S(1)} %fusion.106), channel_id=1, replica_groups=mesh['row'=8,'col'=4] {'row','col'}, use_global_device_ids=true, to_apply=%region_2.2 | all-reduce | flops 4096 | bytes 32768 | tf_op jit(solution)/shard_map/while/body/eval_jaxpr/psum | solution.py:65
  98.4 1.8 fusion.106
  100.2 40.0 %psum.32 = f32[8,512]{1,0:T(8,128)S(1)} all-reduce(f32[8,512]{1,0:T(8,128)S(1)} %fusion.106), channel_id=1, replica_groups=mesh['row'=8,'col'=4] {'row','col'}, use_global_device_ids=true, to_apply=%region_2.2 | all-reduce | flops 4096 | bytes 32768 | tf_op jit(solution)/shard_map/while/body/eval_jaxpr/psum | solution.py:65
  142.9 1.8 fusion.106
  144.7 40.2 %psum.32 = f32[8,512]{1,0:T(8,128)S(1)} all-reduce(f32[8,512]{1,0:T(8,128)S(1)} %fusion.106), channel_id=1, replica_groups=mesh['row'=8,'col'=4] {'row','col'}, use_global_device_ids=true, to_apply=%region_2.2 | all-reduce | flops 4096 | bytes 32768 | tf_op jit(solution)/shard_map/while/body/eval_jaxpr/psum | solution.py:65
  187.6 1.8 fusion.106
  189.4 39.9 %psum.32 = f32[8,512]{1,0:T(8,128)S(1)} all-reduce(f32[8,512]{1,0:T(8,128)S(1)} %fusion.106), channel_id=1, replica_groups=mesh['row'=8,'col'=4] {'row','col'}, use_global_device_ids=true, to_apply=%region_2.2 | all-reduce | flops 4096 | bytes 32768 | tf_op jit(solution)/shard_map/while/body/eval_jaxpr/psum | solution.py:65
  232.0 1.8 fusion.106
  233.8 40.1 %psum.32 = f32[8,512]{1,0:T(8,128)S(1)} all-reduce(f32[8,512]{1,0:T(8,128)S(1)} %fusion.106), channel_id=1, replica_groups=mesh['row'=8,'col'=4] {'row','col'}, use_global_device_ids=true, to_apply=%region_2.2 | all-reduce | flops 4096 | bytes 32768 | tf_op jit(solution)/shard_map/while/body/eval_jaxpr/psum | solution.py:65
  276.7 1.8 fusion.106
  278.5 40.0 %psum.32 = f32[8,512]{1,0:T(8,128)S(1)} all-reduce(f32[8,512]{1,0:T(8,128)S(1)} %fusion.106), channel_id=1, replica_groups=mesh['row'=8,'col'=4] {'row','col'}, use_global_device_ids=true, to_apply=%region_2.2 | all-reduce | flops 4096 | bytes 32768 | tf_op jit(solution)/shard_map/while/body/eval_jaxpr/psum | solution.py:65
  321.2 1.8 fusion.106
  323.0 40.2 %psum.32 = f32[8,512]{1,0:T(8,128)S(1)} all-reduce(f32[8,512]{1,0:T(8,128)S(1)} %fusion.106), channel_id=1, replica_groups=mesh['row'=8,'col'=4] {'row','col'}, use_global_device_ids=true, to_apply=%region_2.2 | all-reduce | flops 4096 | bytes 32768 | tf_op jit(solution)/shard_map/while/body/eval_jaxpr/psum | solution.py:65
  365.9 1.8 fusion.106
  367.7 39.8 %psum.32 = f32[8,512]{1,0:T(8,128)S(1)} all-reduce(f32[8,512]{1,0:T(8,128)S(1)} %fusion.106), channel_id=1, replica_groups=mesh['row'=8,'col'=4] {'row','col'}, use_global_device_ids=true, to_apply=%region_2.2 | all-reduce | flops 4096 | bytes 32768 | tf_op jit(solution)/shard_map/while/body/eval_jaxpr/psum | solution.py:65
  410.2 1.8 fusion.106
  412.0 40.2 %psum.32 = f32[8,512]{1,0:T(8,128)S(1)} all-reduce(f32[8,512]{1,0:T(8,128)S(1)} %fusion.106), channel_id=1, replica_groups=mesh['row'=8,'col'=4] {'row','col'}, use_global_device_ids=true, to_apply=%region_2.2 | all-reduce | flops 4096 | bytes 32768 | tf_op jit(solution)/shard_map/while/body/eval_jaxpr/psum | solution.py:65
  455.0 1.8 fusion.106
  456.7 39.8 %psum.32 = f32[8,512]{1,0:T(8,128)S(1)} all-reduce(f32[8,512]{1,0:T(8,128)S(1)} %fusion.106), channel_id=1, replica_groups=mesh['row'=8,'col'=4] {'row','col'}, use_global_device_ids=true, to_apply=%region_2.2 | all-reduce | flops 4096 | bytes 32768 | tf_op jit(solution)/shard_map/while/body/eval_jaxpr/psum | solution.py:65
  499.3 1.8 fusion.106
  501.1 40.2 %psum.32 = f32[8,512]{1,0:T(8,128)S(1)} all-reduce(f32[8,512]{1,0:T(8,128)S(1)} %fusion.106), channel_id=1, replica_groups=mesh['row'=8,'col'=4] {'row','col'}, use_global_device_ids=true, to_apply=%region_2.2 | all-reduce | flops 4096 | bytes 32768 | tf_op jit(solution)/shard_map/while/body/eval_jaxpr/psum | solution.py:65
  544.0 1.8 fusion.106
  545.8 39.8 %psum.32 = f32[8,512]{1,0:T(8,128)S(1)} all-reduce(f32[8,512]{1,0:T(8,128)S(1)} %fusion.106), channel_id=1, replica_groups=mesh['row'=8,'col'=4] {'row','col'}, use_global_device_ids=true, to_apply=%region_2.2 | all-reduce | flops 4096 | bytes 32768 | tf_op jit(solution)/shard_map/while/body/eval_jaxpr/psum | solution.py:65
  588.3 1.8 fusion.106
  590.1 40.3 %psum.32 = f32[8,512]{1,0:T(8,128)S(1)} all-reduce(f32[8,512]{1,0:T(8,128)S(1)} %fusion.106), channel_id=1, replica_groups=mesh['row'=8,'col'=4] {'row','col'}, use_global_device_ids=true, to_apply=%region_2.2 | all-reduce | flops 4096 | bytes 32768 | tf_op jit(solution)/shard_map/while/body/eval_jaxpr/psum | solution.py:65
  633.2 1.8 fusion.106
  635.0 39.7 %psum.32 = f32[8,512]{1,0:T(8,128)S(1)} all-reduce(f32[8,512]{1,0:T(8,128)S(1)} %fusion.106), channel_id=1, replica_groups=mesh['row'=8,'col'=4] {'row','col'}, use_global_device_ids=true, to_apply=%region_2.2 | all-reduce | flops 4096 | bytes 32768 | tf_op jit(solution)/shard_map/while/body/eval_jaxpr/psum | solution.py:65
  677.4 1.8 fusion.106
  679.2 40.4 %psum.32 = f32[8,512]{1,0:T(8,128)S(1)} all-reduce(f32[8,512]{1,0:T(8,128)S(1)} %fusion.106), channel_id=1, replica_groups=mesh['row'=8,'col'=4] {'row','col'}, use_global_device_ids=true, to_apply=%region_2.2 | all-reduce | flops 4096 | bytes 32768 | tf_op jit(solution)/shard_map/while/body/eval_jaxpr/psum | solution.py:65
  721.8 700.1 %while.33 = (s32[]{:T(128)}, f32[8,16,512]{2,0,1:T(8,128)S(1)}, f32[8,16,512]{2,0,1:T(8,128)S(1)}, s32[2,4]{0,1:T(4,128)S(1)}, s32[]{:T(128)}, /*index=5*/bf16[2...) while((s32[]{:T(128)}, f32[8,16,512]{2,0,1:T(8,128)S(1)}, ...), condition=%wide.region_6.7_spmd.clone, body=%wide.region_4.6_spmd.clone.sunk | while | flops 29382456 | bytes 1203697 | solution.py:99
  724.0 39.6 %psum.33 = f32[8,512]{1,0:T(8,128)S(1)} all-reduce(f32[8,512]{1,0:T(8,128)S(1)} %fusion.113), channel_id=1, replica_groups=mesh['row'=8,'col'=4] {'row','col'}, use_global_device_ids=true, to_apply=%region_5.5 | all-reduce | flops 4096 | bytes 32768 | tf_op jit(solution)/shard_map/while/body/eval_jaxpr/psum | solution.py:93
  767.2 40.5 %psum.33 = f32[8,512]{1,0:T(8,128)S(1)} all-reduce(f32[8,512]{1,0:T(8,128)S(1)} %fusion.113), channel_id=1, replica_groups=mesh['row'=8,'col'=4] {'row','col'}, use_global_device_ids=true, to_apply=%region_5.5 | all-reduce | flops 4096 | bytes 32768 | tf_op jit(solution)/shard_map/while/body/eval_jaxpr/psum | solution.py:93
  807.8 1.5 fusion.114
  811.5 39.5 %psum.33 = f32[8,512]{1,0:T(8,128)S(1)} all-reduce(f32[8,512]{1,0:T(8,128)S(1)} %fusion.113), channel_id=1, replica_groups=mesh['row'=8,'col'=4] {'row','col'}, use_global_device_ids=true, to_apply=%region_5.5 | all-reduce | flops 4096 | bytes 32768 | tf_op jit(solution)/shard_map/while/body/eval_jaxpr/psum | solution.py:93
  851.0 1.5 fusion.114
  854.7 40.6 %psum.33 = f32[8,512]{1,0:T(8,128)S(1)} all-reduce(f32[8,512]{1,0:T(8,128)S(1)} %fusion.113), channel_id=1, replica_groups=mesh['row'=8,'col'=4] {'row','col'}, use_global_device_ids=true, to_apply=%region_5.5 | all-reduce | flops 4096 | bytes 32768 | tf_op jit(solution)/shard_map/while/body/eval_jaxpr/psum | solution.py:93
  895.3 1.5 fusion.114
  899.0 39.4 %psum.33 = f32[8,512]{1,0:T(8,128)S(1)} all-reduce(f32[8,512]{1,0:T(8,128)S(1)} %fusion.113), channel_id=1, replica_groups=mesh['row'=8,'col'=4] {'row','col'}, use_global_device_ids=true, to_apply=%region_5.5 | all-reduce | flops 4096 | bytes 32768 | tf_op jit(solution)/shard_map/while/body/eval_jaxpr/psum | solution.py:93
  938.4 1.5 fusion.114
  942.1 40.7 %psum.33 = f32[8,512]{1,0:T(8,128)S(1)} all-reduce(f32[8,512]{1,0:T(8,128)S(1)} %fusion.113), channel_id=1, replica_groups=mesh['row'=8,'col'=4] {'row','col'}, use_global_device_ids=true, to_apply=%region_5.5 | all-reduce | flops 4096 | bytes 32768 | tf_op jit(solution)/shard_map/while/body/eval_jaxpr/psum | solution.py:93
  982.8 1.5 fusion.114
  986.5 39.4 %psum.33 = f32[8,512]{1,0:T(8,128)S(1)} all-reduce(f32[8,512]{1,0:T(8,128)S(1)} %fusion.113), channel_id=1, replica_groups=mesh['row'=8,'col'=4] {'row','col'}, use_global_device_ids=true, to_apply=%region_5.5 | all-reduce | flops 4096 | bytes 32768 | tf_op jit(solution)/shard_map/while/body/eval_jaxpr/psum | solution.py:93
  1026.0 1.5 fusion.114
  1029.6 40.7 %psum.33 = f32[8,512]{1,0:T(8,128)S(1)} all-reduce(f32[8,512]{1,0:T(8,128)S(1)} %fusion.113), channel_id=1, replica_groups=mesh['row'=8,'col'=4] {'row','col'}, use_global_device_ids=true, to_apply=%region_5.5 | all-reduce | flops 4096 | bytes 32768 | tf_op jit(solution)/shard_map/while/body/eval_jaxpr/psum | solution.py:93
  1070.3 1.5 fusion.114
  1074.0 39.4 %psum.33 = f32[8,512]{1,0:T(8,128)S(1)} all-reduce(f32[8,512]{1,0:T(8,128)S(1)} %fusion.113), channel_id=1, replica_groups=mesh['row'=8,'col'=4] {'row','col'}, use_global_device_ids=true, to_apply=%region_5.5 | all-reduce | flops 4096 | bytes 32768 | tf_op jit(solution)/shard_map/while/body/eval_jaxpr/psum | solution.py:93
  1113.5 1.5 fusion.114
  1117.1 40.7 %psum.33 = f32[8,512]{1,0:T(8,128)S(1)} all-reduce(f32[8,512]{1,0:T(8,128)S(1)} %fusion.113), channel_id=1, replica_groups=mesh['row'=8,'col'=4] {'row','col'}, use_global_device_ids=true, to_apply=%region_5.5 | all-reduce | flops 4096 | bytes 32768 | tf_op jit(solution)/shard_map/while/body/eval_jaxpr/psum | solution.py:93
  1157.8 1.5 fusion.114
  1161.5 39.4 %psum.33 = f32[8,512]{1,0:T(8,128)S(1)} all-reduce(f32[8,512]{1,0:T(8,128)S(1)} %fusion.113), channel_id=1, replica_groups=mesh['row'=8,'col'=4] {'row','col'}, use_global_device_ids=true, to_apply=%region_5.5 | all-reduce | flops 4096 | bytes 32768 | tf_op jit(solution)/shard_map/while/body/eval_jaxpr/psum | solution.py:93
  1201.0 1.5 fusion.114
  1204.6 40.7 %psum.33 = f32[8,512]{1,0:T(8,128)S(1)} all-reduce(f32[8,512]{1,0:T(8,128)S(1)} %fusion.113), channel_id=1, replica_groups=mesh['row'=8,'col'=4] {'row','col'}, use_global_device_ids=true, to_apply=%region_5.5 | all-reduce | flops 4096 | bytes 32768 | tf_op jit(solution)/shard_map/while/body/eval_jaxpr/psum | solution.py:93
  1245.3 1.5 fusion.114
  1249.0 39.4 %psum.33 = f32[8,512]{1,0:T(8,128)S(1)} all-reduce(f32[8,512]{1,0:T(8,128)S(1)} %fusion.113), channel_id=1, replica_groups=mesh['row'=8,'col'=4] {'row','col'}, use_global_device_ids=true, to_apply=%region_5.5 | all-reduce | flops 4096 | bytes 32768 | tf_op jit(solution)/shard_map/while/body/eval_jaxpr/psum | solution.py:93
  1288.5 1.5 fusion.114
  1292.2 40.7 %psum.33 = f32[8,512]{1,0:T(8,128)S(1)} all-reduce(f32[8,512]{1,0:T(8,128)S(1)} %fusion.113), channel_id=1, replica_groups=mesh['row'=8,'col'=4] {'row','col'}, use_global_device_ids=true, to_apply=%region_5.5 | all-reduce | flops 4096 | bytes 32768 | tf_op jit(solution)/shard_map/while/body/eval_jaxpr/psum | solution.py:93
  1332.8 1.5 fusion.114
  1336.5 39.4 %psum.33 = f32[8,512]{1,0:T(8,128)S(1)} all-reduce(f32[8,512]{1,0:T(8,128)S(1)} %fusion.113), channel_id=1, replica_groups=mesh['row'=8,'col'=4] {'row','col'}, use_global_device_ids=true, to_apply=%region_5.5 | all-reduce | flops 4096 | bytes 32768 | tf_op jit(solution)/shard_map/while/body/eval_jaxpr/psum | solution.py:93
  1376.0 1.5 fusion.114
  1379.7 40.7 %psum.33 = f32[8,512]{1,0:T(8,128)S(1)} all-reduce(f32[8,512]{1,0:T(8,128)S(1)} %fusion.113), channel_id=1, replica_groups=mesh['row'=8,'col'=4] {'row','col'}, use_global_device_ids=true, to_apply=%region_5.5 | all-reduce | flops 4096 | bytes 32768 | tf_op jit(solution)/shard_map/while/body/eval_jaxpr/psum | solution.py:93
  (246 shorter events, 88.7 us)
Async XLA Ops:
  0.6 1422.8 %copy-start = (bf16[1,512,512]{2,1,0:T(8,128)(2,1)S(1)}, bf16[1,512,512]{2,1,0:T(8,128)(2,1)}, u32[]{:S(2)}) copy-start(bf16[1,512,512]{2,1,0:T(8,128)(2,1)} %param.20) | copy-start | bytes 1572868
  5.7 1417.3 %copy-start.1 = (bf16[1,512,1024]{2,1,0:T(8,128)(2,1)S(1)}, bf16[1,512,1024]{2,1,0:T(8,128)(2,1)}, u32[]{:S(2)}) copy-start(bf16[1,512,1024]{2,1,0:T(8,128)(2,1)} %param.19) | copy-start | bytes 3145732
  5.8 1417.7 %copy-start.2 = (bf16[1,8,512]{2,1,0:T(8,128)(2,1)S(1)}, bf16[1,8,512]{2,1,0:T(8,128)(2,1)}, u32[]{:S(2)}) copy-start(bf16[1,8,512]{2,1,0:T(8,128)(2,1)} %param.18) | copy-start | bytes 24580
where the time goes:
time: 1430 us; the launch traced here: 1420 us
  blocking collectives  1280 us (90%)
  matrix products  100 us (7%)
  local copies, waits for them, and re-layouts  33.4 us (2%)
    psum x16, blocking collectives, forward(): row_total = lax.psum(partial_value + carried, ('row', 'col'))  643 us
    psum x16, blocking collectives, backward(): col_total = lax.psum(partial_value, ('row', 'col'))  641 us

commit v1 on v0

--- a/solution.py
+++ b/solution.py
@@ -62,7 +62,8 @@
             "rbq,bqt->rt", coefficient_values, left_row_index, preferred_element_type=jnp.float32
         )
         carried = lax.dynamic_index_in_dim(dense_sum, column, 1, keepdims=False)
-        row_total = lax.psum(partial_value + carried, ("row", "col"))
+        obj = partial_value + carried
+        row_total = lax.psum(lax.psum(obj, axis_name="col"), axis_name="row")
         block_rhs = lax.dynamic_index_in_dim(right_side, column, 1, keepdims=False).astype(
             jnp.float32
         )

time: 1430 us -> 1480 us (1.035)
  blocking collectives: 1280 us -> 1330 us
    psum x16 -> x32, blocking collectives: 643 us -> 696 us  [forward(): row_total = lax.psum(lax.psum(obj, axis_name='col'), axis_name='row')]
where the time goes in v1:
time: 1480 us
  blocking collectives  1330 us (90%)
  matrix products  100 us (7%)
  local copies, waits for them, and re-layouts  33.4 us (2%)
    psum x32, blocking collectives, forward(): row_total = lax.psum(lax.psum(obj, axis_name='col'), axis_name='row')  696 us
    psum x16, blocking collectives, backward(): col_total = lax.psum(partial_value, ('row', 'col'))  638 us

profile of v1, /device:TPU:0, one launch (start us, length us, event | category | flops | bytes accessed | tf_op | source)
XLA Modules:
  0.0 1475.4 jit_solution(7232808089595948276)
XLA Ops:
  5.8 768.7 %while.32 = (s32[]{:T(128)}, f32[8,16,512]{2,0,1:T(8,128)S(1)}, bf16[8,16,512]{2,1,0:T(8,128)(2,1)S(1)}, s32[2,4]{1,0:T(2,128)}, s32[]{:T(128)}, /*index=5*/bf16...) while((s32[]{:T(128)}, f32[8,16,512]{2,0,1:T(8,128)S(1)}, ...), condition=%wide.region_4.5_spmd.clone, body=%wide.region_1.4_spmd.clone.sunk | while | flops 33602120 | bytes 1851328 | solution.py:74
  7.2 1.8 fusion.106
  9.0 12.7 psum.48
  21.7 37.4 %psum.49 = f32[8,512]{1,0:T(8,128)S(1)} all-reduce(f32[8,512]{1,0:T(8,128)S(1)} %psum.48), channel_id=1, replica_groups=mesh['row'=8,'col'=4] {'row'}, use_global_device_ids=true, to_apply=%region_3.3 | all-reduce | flops 4096 | bytes 32768 | tf_op jit(solution)/shard_map/while/body/eval_jaxpr/psum | solution.py:66
  61.8 1.8 fusion.106
  63.6 10.2 psum.48
  73.8 33.0 %psum.49 = f32[8,512]{1,0:T(8,128)S(1)} all-reduce(f32[8,512]{1,0:T(8,128)S(1)} %psum.48), channel_id=1, replica_groups=mesh['row'=8,'col'=4] {'row'}, use_global_device_ids=true, to_apply=%region_3.3 | all-reduce | flops 4096 | bytes 32768 | tf_op jit(solution)/shard_map/while/body/eval_jaxpr/psum | solution.py:66
  111.3 10.1 psum.48
  121.4 33.0 %psum.49 = f32[8,512]{1,0:T(8,128)S(1)} all-reduce(f32[8,512]{1,0:T(8,128)S(1)} %psum.48), channel_id=1, replica_groups=mesh['row'=8,'col'=4] {'row'}, use_global_device_ids=true, to_apply=%region_3.3 | all-reduce | flops 4096 | bytes 32768 | tf_op jit(solution)/shard_map/while/body/eval_jaxpr/psum | solution.py:66
  157.1 1.8 fusion.106
  158.9 10.1 psum.48
  169.0 33.0 %psum.49 = f32[8,512]{1,0:T(8,128)S(1)} all-reduce(f32[8,512]{1,0:T(8,128)S(1)} %psum.48), channel_id=1, replica_groups=mesh['row'=8,'col'=4] {'row'}, use_global_device_ids=true, to_apply=%region_3.3 | all-reduce | flops 4096 | bytes 32768 | tf_op jit(solution)/shard_map/while/body/eval_jaxpr/psum | solution.py:66
  204.7 1.8 fusion.106
  206.5 10.1 psum.48
  216.6 33.0 %psum.49 = f32[8,512]{1,0:T(8,128)S(1)} all-reduce(f32[8,512]{1,0:T(8,128)S(1)} %psum.48), channel_id=1, replica_groups=mesh['row'=8,'col'=4] {'row'}, use_global_device_ids=true, to_apply=%region_3.3 | all-reduce | flops 4096 | bytes 32768 | tf_op jit(solution)/shard_map/while/body/eval_jaxpr/psum | solution.py:66
  254.1 10.1 psum.48
  264.2 33.0 %psum.49 = f32[8,512]{1,0:T(8,128)S(1)} all-reduce(f32[8,512]{1,0:T(8,128)S(1)} %psum.48), channel_id=1, replica_groups=mesh['row'=8,'col'=4] {'row'}, use_global_device_ids=true, to_apply=%region_3.3 | all-reduce | flops 4096 | bytes 32768 | tf_op jit(solution)/shard_map/while/body/eval_jaxpr/psum | solution.py:66
  299.9 1.8 fusion.106
  301.7 10.1 psum.48
  311.8 33.0 %psum.49 = f32[8,512]{1,0:T(8,128)S(1)} all-reduce(f32[8,512]{1,0:T(8,128)S(1)} %psum.48), channel_id=1, replica_groups=mesh['row'=8,'col'=4] {'row'}, use_global_device_ids=true, to_apply=%region_3.3 | all-reduce | flops 4096 | bytes 32768 | tf_op jit(solution)/shard_map/while/body/eval_jaxpr/psum | solution.py:66
  347.5 1.8 fusion.106
  349.3 10.1 psum.48
  359.4 33.0 %psum.49 = f32[8,512]{1,0:T(8,128)S(1)} all-reduce(f32[8,512]{1,0:T(8,128)S(1)} %psum.48), channel_id=1, replica_groups=mesh['row'=8,'col'=4] {'row'}, use_global_device_ids=true, to_apply=%region_3.3 | all-reduce | flops 4096 | bytes 32768 | tf_op jit(solution)/shard_map/while/body/eval_jaxpr/psum | solution.py:66
  395.1 1.8 fusion.106
  396.9 10.1 psum.48
  407.0 33.0 %psum.49 = f32[8,512]{1,0:T(8,128)S(1)} all-reduce(f32[8,512]{1,0:T(8,128)S(1)} %psum.48), channel_id=1, replica_groups=mesh['row'=8,'col'=4] {'row'}, use_global_device_ids=true, to_apply=%region_3.3 | all-reduce | flops 4096 | bytes 32768 | tf_op jit(solution)/shard_map/while/body/eval_jaxpr/psum | solution.py:66
  442.7 1.8 fusion.106
  444.5 10.1 psum.48
  454.6 33.0 %psum.49 = f32[8,512]{1,0:T(8,128)S(1)} all-reduce(f32[8,512]{1,0:T(8,128)S(1)} %psum.48), channel_id=1, replica_groups=mesh['row'=8,'col'=4] {'row'}, use_global_device_ids=true, to_apply=%region_3.3 | all-reduce | flops 4096 | bytes 32768 | tf_op jit(solution)/shard_map/while/body/eval_jaxpr/psum | solution.py:66
  490.3 1.8 fusion.106
  492.1 10.1 psum.48
  502.2 33.0 %psum.49 = f32[8,512]{1,0:T(8,128)S(1)} all-reduce(f32[8,512]{1,0:T(8,128)S(1)} %psum.48), channel_id=1, replica_groups=mesh['row'=8,'col'=4] {'row'}, use_global_device_ids=true, to_apply=%region_3.3 | all-reduce | flops 4096 | bytes 32768 | tf_op jit(solution)/shard_map/while/body/eval_jaxpr/psum | solution.py:66
  537.9 1.8 fusion.106
  539.7 10.1 psum.48
  549.8 33.0 %psum.49 = f32[8,512]{1,0:T(8,128)S(1)} all-reduce(f32[8,512]{1,0:T(8,128)S(1)} %psum.48), channel_id=1, replica_groups=mesh['row'=8,'col'=4] {'row'}, use_global_device_ids=true, to_apply=%region_3.3 | all-reduce | flops 4096 | bytes 32768 | tf_op jit(solution)/shard_map/while/body/eval_jaxpr/psum | solution.py:66
  585.5 1.8 fusion.106
  587.3 10.1 psum.48
  597.4 33.0 %psum.49 = f32[8,512]{1,0:T(8,128)S(1)} all-reduce(f32[8,512]{1,0:T(8,128)S(1)} %psum.48), channel_id=1, replica_groups=mesh['row'=8,'col'=4] {'row'}, use_global_device_ids=true, to_apply=%region_3.3 | all-reduce | flops 4096 | bytes 32768 | tf_op jit(solution)/shard_map/while/body/eval_jaxpr/psum | solution.py:66
  633.1 1.8 fusion.106
  634.8 10.1 psum.48
  645.0 33.0 %psum.49 = f32[8,512]{1,0:T(8,128)S(1)} all-reduce(f32[8,512]{1,0:T(8,128)S(1)} %psum.48), channel_id=1, replica_groups=mesh['row'=8,'col'=4] {'row'}, use_global_device_ids=true, to_apply=%region_3.3 | all-reduce | flops 4096 | bytes 32768 | tf_op jit(solution)/shard_map/while/body/eval_jaxpr/psum | solution.py:66
  680.7 1.8 fusion.106
  682.4 10.1 psum.48
  692.6 33.0 %psum.49 = f32[8,512]{1,0:T(8,128)S(1)} all-reduce(f32[8,512]{1,0:T(8,128)S(1)} %psum.48), channel_id=1, replica_groups=mesh['row'=8,'col'=4] {'row'}, use_global_device_ids=true, to_apply=%region_3.3 | all-reduce | flops 4096 | bytes 32768 | tf_op jit(solution)/shard_map/while/body/eval_jaxpr/psum | solution.py:66
  728.3 1.8 fusion.106
  730.0 10.1 psum.48
  740.1 33.0 %psum.49 = f32[8,512]{1,0:T(8,128)S(1)} all-reduce(f32[8,512]{1,0:T(8,128)S(1)} %psum.48), channel_id=1, replica_groups=mesh['row'=8,'col'=4] {'row'}, use_global_device_ids=true, to_apply=%region_3.3 | all-reduce | flops 4096 | bytes 32768 | tf_op jit(solution)/shard_map/while/body/eval_jaxpr/psum | solution.py:66
  775.3 697.6 %while.33 = (s32[]{:T(128)}, f32[8,16,512]{2,0,1:T(8,128)S(1)}, f32[8,16,512]{2,0,1:T(8,128)S(1)}, s32[2,4]{0,1:T(4,128)S(1)}, s32[]{:T(128)}, /*index=5*/bf16[2...) while((s32[]{:T(128)}, f32[8,16,512]{2,0,1:T(8,128)S(1)}, ...), condition=%wide.region_7.8_spmd.clone, body=%wide.region_5.7_spmd.clone.sunk | while | flops 29382456 | bytes 1203697 | solution.py:100
  777.5 36.9 %psum.50 = f32[8,512]{1,0:T(8,128)S(1)} all-reduce(f32[8,512]{1,0:T(8,128)S(1)} %fusion.113), channel_id=1, replica_groups=mesh['row'=8,'col'=4] {'row','col'}, use_global_device_ids=true, to_apply=%region_6.6 | all-reduce | flops 4096 | bytes 32768 | tf_op jit(solution)/shard_map/while/body/eval_jaxpr/psum | solution.py:94
  818.1 41.3 %psum.50 = f32[8,512]{1,0:T(8,128)S(1)} all-reduce(f32[8,512]{1,0:T(8,128)S(1)} %fusion.113), channel_id=1, replica_groups=mesh['row'=8,'col'=4] {'row','col'}, use_global_device_ids=true, to_apply=%region_6.6 | all-reduce | flops 4096 | bytes 32768 | tf_op jit(solution)/shard_map/while/body/eval_jaxpr/psum | solution.py:94
  863.0 39.5 %psum.50 = f32[8,512]{1,0:T(8,128)S(1)} all-reduce(f32[8,512]{1,0:T(8,128)S(1)} %fusion.113), channel_id=1, replica_groups=mesh['row'=8,'col'=4] {'row','col'}, use_global_device_ids=true, to_apply=%region_6.6 | all-reduce | flops 4096 | bytes 32768 | tf_op jit(solution)/shard_map/while/body/eval_jaxpr/psum | solution.py:94
  906.2 40.5 %psum.50 = f32[8,512]{1,0:T(8,128)S(1)} all-reduce(f32[8,512]{1,0:T(8,128)S(1)} %fusion.113), channel_id=1, replica_groups=mesh['row'=8,'col'=4] {'row','col'}, use_global_device_ids=true, to_apply=%region_6.6 | all-reduce | flops 4096 | bytes 32768 | tf_op jit(solution)/shard_map/while/body/eval_jaxpr/psum | solution.py:94
  950.4 39.5 %psum.50 = f32[8,512]{1,0:T(8,128)S(1)} all-reduce(f32[8,512]{1,0:T(8,128)S(1)} %fusion.113), channel_id=1, replica_groups=mesh['row'=8,'col'=4] {'row','col'}, use_global_device_ids=true, to_apply=%region_6.6 | all-reduce | flops 4096 | bytes 32768 | tf_op jit(solution)/shard_map/while/body/eval_jaxpr/psum | solution.py:94
  993.6 40.5 %psum.50 = f32[8,512]{1,0:T(8,128)S(1)} all-reduce(f32[8,512]{1,0:T(8,128)S(1)} %fusion.113), channel_id=1, replica_groups=mesh['row'=8,'col'=4] {'row','col'}, use_global_device_ids=true, to_apply=%region_6.6 | all-reduce | flops 4096 | bytes 32768 | tf_op jit(solution)/shard_map/while/body/eval_jaxpr/psum | solution.py:94
  1037.8 39.6 %psum.50 = f32[8,512]{1,0:T(8,128)S(1)} all-reduce(f32[8,512]{1,0:T(8,128)S(1)} %fusion.113), channel_id=1, replica_groups=mesh['row'=8,'col'=4] {'row','col'}, use_global_device_ids=true, to_apply=%region_6.6 | all-reduce | flops 4096 | bytes 32768 | tf_op jit(solution)/shard_map/while/body/eval_jaxpr/psum | solution.py:94
  1081.1 40.5 %psum.50 = f32[8,512]{1,0:T(8,128)S(1)} all-reduce(f32[8,512]{1,0:T(8,128)S(1)} %fusion.113), channel_id=1, replica_groups=mesh['row'=8,'col'=4] {'row','col'}, use_global_device_ids=true, to_apply=%region_6.6 | all-reduce | flops 4096 | bytes 32768 | tf_op jit(solution)/shard_map/while/body/eval_jaxpr/psum | solution.py:94
  1125.3 39.6 %psum.50 = f32[8,512]{1,0:T(8,128)S(1)} all-reduce(f32[8,512]{1,0:T(8,128)S(1)} %fusion.113), channel_id=1, replica_groups=mesh['row'=8,'col'=4] {'row','col'}, use_global_device_ids=true, to_apply=%region_6.6 | all-reduce | flops 4096 | bytes 32768 | tf_op jit(solution)/shard_map/while/body/eval_jaxpr/psum | solution.py:94
  1168.5 40.5 %psum.50 = f32[8,512]{1,0:T(8,128)S(1)} all-reduce(f32[8,512]{1,0:T(8,128)S(1)} %fusion.113), channel_id=1, replica_groups=mesh['row'=8,'col'=4] {'row','col'}, use_global_device_ids=true, to_apply=%region_6.6 | all-reduce | flops 4096 | bytes 32768 | tf_op jit(solution)/shard_map/while/body/eval_jaxpr/psum | solution.py:94
  1212.7 39.6 %psum.50 = f32[8,512]{1,0:T(8,128)S(1)} all-reduce(f32[8,512]{1,0:T(8,128)S(1)} %fusion.113), channel_id=1, replica_groups=mesh['row'=8,'col'=4] {'row','col'}, use_global_device_ids=true, to_apply=%region_6.6 | all-reduce | flops 4096 | bytes 32768 | tf_op jit(solution)/shard_map/while/body/eval_jaxpr/psum | solution.py:94
  1255.9 40.5 %psum.50 = f32[8,512]{1,0:T(8,128)S(1)} all-reduce(f32[8,512]{1,0:T(8,128)S(1)} %fusion.113), channel_id=1, replica_groups=mesh['row'=8,'col'=4] {'row','col'}, use_global_device_ids=true, to_apply=%region_6.6 | all-reduce | flops 4096 | bytes 32768 | tf_op jit(solution)/shard_map/while/body/eval_jaxpr/psum | solution.py:94
  1300.1 39.6 %psum.50 = f32[8,512]{1,0:T(8,128)S(1)} all-reduce(f32[8,512]{1,0:T(8,128)S(1)} %fusion.113), channel_id=1, replica_groups=mesh['row'=8,'col'=4] {'row','col'}, use_global_device_ids=true, to_apply=%region_6.6 | all-reduce | flops 4096 | bytes 32768 | tf_op jit(solution)/shard_map/while/body/eval_jaxpr/psum | solution.py:94
  1343.3 40.6 %psum.50 = f32[8,512]{1,0:T(8,128)S(1)} all-reduce(f32[8,512]{1,0:T(8,128)S(1)} %fusion.113), channel_id=1, replica_groups=mesh['row'=8,'col'=4] {'row','col'}, use_global_device_ids=true, to_apply=%region_6.6 | all-reduce | flops 4096 | bytes 32768 | tf_op jit(solution)/shard_map/while/body/eval_jaxpr/psum | solution.py:94
  1387.6 39.5 %psum.50 = f32[8,512]{1,0:T(8,128)S(1)} all-reduce(f32[8,512]{1,0:T(8,128)S(1)} %fusion.113), channel_id=1, replica_groups=mesh['row'=8,'col'=4] {'row','col'}, use_global_device_ids=true, to_apply=%region_6.6 | all-reduce | flops 4096 | bytes 32768 | tf_op jit(solution)/shard_map/while/body/eval_jaxpr/psum | solution.py:94
  1430.8 40.6 %psum.50 = f32[8,512]{1,0:T(8,128)S(1)} all-reduce(f32[8,512]{1,0:T(8,128)S(1)} %fusion.113), channel_id=1, replica_groups=mesh['row'=8,'col'=4] {'row','col'}, use_global_device_ids=true, to_apply=%region_6.6 | all-reduce | flops 4096 | bytes 32768 | tf_op jit(solution)/shard_map/while/body/eval_jaxpr/psum | solution.py:94
  (262 shorter events, 113.8 us)
Async XLA Ops:
  0.6 1473.8 %copy-start = (bf16[1,512,512]{2,1,0:T(8,128)(2,1)S(1)}, bf16[1,512,512]{2,1,0:T(8,128)(2,1)}, u32[]{:S(2)}) copy-start(bf16[1,512,512]{2,1,0:T(8,128)(2,1)} %param.20) | copy-start | bytes 1572868
  5.7 1468.4 %copy-start.1 = (bf16[1,512,1024]{2,1,0:T(8,128)(2,1)S(1)}, bf16[1,512,1024]{2,1,0:T(8,128)(2,1)}, u32[]{:S(2)}) copy-start(bf16[1,512,1024]{2,1,0:T(8,128)(2,1)} %param.19) | copy-start | bytes 3145732
  5.8 1468.7 %copy-start.2 = (bf16[1,8,512]{2,1,0:T(8,128)(2,1)S(1)}, bf16[1,8,512]{2,1,0:T(8,128)(2,1)}, u32[]{:S(2)}) copy-start(bf16[1,8,512]{2,1,0:T(8,128)(2,1)} %param.18) | copy-start | bytes 24580
